TPU v7x, 8 devices: a whole 2x2x1 slice. The times are simulated.
8 devices in a mesh: rep: 2 (over z, y), vocab: 4 (over x, core).
Axes of the slice: x: 2, y: 2, z: 1, core: 2. Of those that a mesh axis runs over, the one named last changes fastest.
Arguments:
- hidden: bfloat16 [512, 5120], P(('rep', 'vocab')), parts along dimension 0
- w_head: bfloat16 [131072, 5120], P('vocab')
- allowed_ids: int32 [4096], P('rep'), parts along dimension 0
- allowed_valid: int32 [4096], P('rep'), parts along dimension 0
- target_pos: int32 [512], P(('rep', 'vocab')), parts along dimension 0
Outputs:
- output 1: float32 [512, 2048], P(('rep', 'vocab')), parts along dimension 0
- output 2: float32 [512], P(('rep', 'vocab')), parts along dimension 0
There are 2 independent parts. A program takes and returns all parts, laid end to end along the dimension named above; an argument that names none is the same for every part.
All inputs are finite; a program needn't handle non-finite values.
Results may differ from a plain program's by a relative error of at most 0.001.
Values are sent between devices in bfloat16 or wider.
A program may use at most 1.5 GiB of HBM per device.

v0:
```python
import functools

import jax
import jax.numpy as jnp
from jax import lax
from jax.experimental import pallas as pl
from jax.experimental.pallas import tpu as pltpu
from jax.sharding import PartitionSpec as P

INV_TEMP = 1.25
MESH = pl.DeviceIdType.MESH
LANES = 128
TILE_ROWS = 8
MIB = 1 << 20
ISSUE = 8
PARTS = 4


def listed(keys, limit):
    length = keys.shape[0]
    low = jnp.int32(0)
    step = length
    while step:
        probe = low + step
        below = keys[jnp.minimum(probe, length) - 1] < limit
        low = jnp.where(below & (probe <= length), probe, low)
        step //= 2
    return low


def gather_kernel(keys, w, pairs, sem, *, row_bits):
    length = keys.shape[0]
    n_groups = lax.div(listed(keys, length << row_bits) + ISSUE - 1, ISSUE)

    def issue(i, carry):
        for u in range(ISSUE):
            key = keys[i * ISSUE + u]
            row = lax.bitwise_and(key, (1 << row_bits) - 1)
            src = w.at[lax.shift_right_logical(row, 3), :, lax.bitwise_and(lax.shift_right_logical(row, 1), 3)]
            spot = lax.bitwise_and(lax.shift_right_logical(key, row_bits), length - 1)
            pltpu.make_async_copy(src, pairs.at[:, spot], sem).start()
        return carry

    lax.fori_loop(0, n_groups, issue, 0)

    def wait(i, carry):
        group = pairs.at[:, pl.ds(0, ISSUE)]
        pltpu.make_async_copy(group, group, sem).wait()
        return carry

    lax.fori_loop(0, n_groups, wait, 0)


def score_kernel(code, rows, h_own, h_pair, h_far, h_far_pair, valid, target, probs, logp, hidden, both, give_near, give_far,
                 pair_near, pair_far, near, far_send, far_recv, turned, scores, gf_s, gf_r, gn_s, gn_r, x_s, x_r, t_s, t_r):
    me = lax.axis_index('vocab')
    core = lax.rem(me, 2)
    partner = me + 1 - 2 * core
    far = me + 2 - 4 * lax.div(me, 2)
    length = valid.shape[1]
    half = length // 2
    part = half // PARTS
    rows_dev = probs.shape[0]
    ktiles = rows.shape[0]

    barrier = pltpu.get_barrier_semaphore()
    for peer in (partner, far):
        pl.semaphore_signal(barrier, inc=1, device_id={'vocab': peer}, device_id_type=MESH)
    for src, which in ((h_own, core), (h_pair, 1 - core), (h_far, 2 + core), (h_far_pair, 3 - core)):
        hidden[pl.ds(pl.multiple_of(which * rows_dev, rows_dev), rows_dev), :] = src[...]
    pl.semaphore_wait(barrier, 2)

    def remote(src, dst, s, r, peer):
        return pltpu.make_async_remote_copy(src_ref=src, dst_ref=dst, send_sem=s, recv_sem=r, device_id={'vocab': peer}, device_id_type=MESH)

    def give_far_copy(q):
        return remote(give_far.at[q], pair_far.at[q], gf_s.at[q], gf_r.at[q], partner)

    def give_near_copy(q):
        return remote(give_near.at[q], pair_near.at[q], gn_s.at[q], gn_r.at[q], partner)

    def far_copy(q):
        return remote(far_send.at[q], far_recv.at[q], x_s.at[q], x_r.at[q], far)

    def turn_copy(q):
        src = turned.at[q, pl.ds(pl.multiple_of((1 - core) * rows_dev, rows_dev), rows_dev)]
        return remote(src, scores.at[core, :, pl.ds(pl.multiple_of(q * part, part), part)], t_s.at[q], t_r.at[q], partner)

    def part_scores(start):
        at = pl.ds(pl.multiple_of(2 * start, 2 * part), 2 * part)
        acc = jnp.zeros((2 * part, 2 * LANES), jnp.float32)
        for k in range(0, ktiles, 2):
            lhs = jnp.concatenate([rows[k, at], rows[k + 1, at]], axis=1)
            acc += lax.dot_general(lhs, hidden[:, k * LANES:(k + 2) * LANES], (((1,), (1,)), ((), ())), preferred_element_type=jnp.float32)
        both[0] = acc[:, :LANES]
        both[1] = acc[:, LANES:]
        kind = jnp.broadcast_to(code[:, pl.ds(pl.multiple_of(start, part), part)], (LANES, part)).T
        picked = []
        for side in range(2):
            even = both[side, pl.ds(0, part, 2), :]
            odd = both[side, pl.ds(1, part, 2), :]
            picked.append(jnp.where(kind == 2, odd, jnp.where(kind == 1, even, 0.0)))
        return picked

    def step(q, carry):
        near_part, far_part = part_scores((1 - core) * half + q * part)
        give_far[q] = far_part
        give_far_copy(q).start()
        give_near[q] = near_part
        give_near_copy(q).start()
        near_part, far_part = part_scores(core * half + q * part)
        give_far_copy(q).wait_recv()
        far_send[q] = far_part + pair_far[q]
        far_copy(q).start()
        give_near_copy(q).wait_recv()
        near[q] = near_part + pair_near[q]
        return carry

    lax.fori_loop(0, PARTS, step, 0)
    for q in range(PARTS):
        far_copy(q).wait_recv()
        turned[q] = (near[q] + far_recv[q]).T * INV_TEMP
        turn_copy(q).start()
        scores[core, :, q * part:(q + 1) * part] = turned[q, pl.ds(pl.multiple_of(core * rows_dev, rows_dev), rows_dev)]
    for q in range(PARTS):
        turn_copy(q).wait_recv()

    s = jnp.concatenate([scores[0], scores[1]], axis=1)
    keep = jnp.broadcast_to(valid[...] > 0, s.shape)
    top = jnp.max(jnp.where(keep, s, -jnp.inf), axis=1, keepdims=True)
    total = jnp.sum(jnp.where(keep, jnp.exp(s - top), 0.0), axis=1, keepdims=True)
    log_norm = top + jnp.log(total)
    probs[...] = jnp.where(keep, jnp.exp(s - log_norm), 0.0)
    wanted = jnp.broadcast_to(target[...], (LANES, rows_dev)).T[:, :1]
    hit = lax.broadcasted_iota(jnp.int32, s.shape, 1) == wanted
    picked = jnp.sum(jnp.where(hit, s, 0.0), axis=1, keepdims=True) - log_norm
    logp[...] = jnp.broadcast_to(picked, (rows_dev, LANES)).T[:1, :]
    for q in range(PARTS):
        give_far_copy(q).wait_send()
        give_near_copy(q).wait_send()
        far_copy(q).wait_send()
        turn_copy(q).wait_send()


def solution(mesh):
    shards = mesh.shape['vocab']
    across = [(i, i ^ 2) for i in range(shards)]
    beside = [(i, i ^ 1) for i in range(shards)]

    def device_step(hidden, w_head, allowed_ids, allowed_valid, target_pos):
        rows_dev, depth = hidden.shape
        vocab_local = w_head.shape[0]
        length = allowed_ids.shape[0]
        row_bits = vocab_local.bit_length() - 1
        width = rows_dev * shards
        ktiles = depth // LANES
        h_far = lax.ppermute(hidden, 'vocab', across)
        h_pair = lax.ppermute(hidden, 'vocab', beside)

        me = lax.axis_index('vocab')
        mine = (lax.shift_right_logical(allowed_ids, row_bits) == me) & (allowed_valid > 0)
        places = jnp.arange(length, dtype=jnp.int32)
        keys = lax.sort(jnp.where(mine, places, places + length) * vocab_local + lax.bitwise_and(allowed_ids, vocab_local - 1))
        code = jnp.where(mine, 1 + lax.bitwise_and(allowed_ids, 1), 0).reshape(1, length)

        target = target_pos.reshape(1, rows_dev)
        keys, code, target, h_pair = lax.optimization_barrier((keys, code, target, h_pair))

        w_view = w_head.reshape(vocab_local // TILE_ROWS, TILE_ROWS, ktiles, LANES).transpose(0, 2, 1, 3).reshape(vocab_local // TILE_ROWS, ktiles, TILE_ROWS // 2, 2, LANES)
        any_spec = pl.BlockSpec(memory_space=pl.ANY)
        smem_spec = pl.BlockSpec(memory_space=pltpu.SMEM)
        vmem_spec = pl.BlockSpec(memory_space=pltpu.VMEM)
        pairs = pl.pallas_call(
            functools.partial(gather_kernel, row_bits=row_bits),
            out_shape=pltpu.VMEM((ktiles, length, 2, LANES), jnp.bfloat16),
            in_specs=[smem_spec, any_spec],
            out_specs=vmem_spec,
            scratch_shapes=[pltpu.SemaphoreType.DMA],
            compiler_params=pltpu.CompilerParams(vmem_limit_bytes=2 * MIB),
        )(keys, w_view)
        h_far, pairs = lax.optimization_barrier((h_far, pairs))
        h_far_pair = lax.ppermute(h_far, 'vocab', beside)
        pair_rows = pltpu.with_memory_space_constraint(pairs.reshape(ktiles, 2 * length, LANES), pltpu.VMEM)
        part = length // 2 // PARTS
        probs, logp = pl.pallas_call(
            score_kernel,
            out_shape=(pltpu.VMEM((rows_dev, length), jnp.float32), jax.ShapeDtypeStruct((1, rows_dev), jnp.float32)),
            in_specs=[vmem_spec] * 8,
            out_specs=(vmem_spec, vmem_spec),
            scratch_shapes=[pltpu.VMEM((width, depth), jnp.bfloat16), pltpu.VMEM((2, 2 * part, LANES), jnp.float32)]
            + [pltpu.VMEM((PARTS, part, LANES), jnp.float32)] * 7
            + [pltpu.VMEM((PARTS, LANES, part), jnp.float32), pltpu.VMEM((2, rows_dev, length // 2), jnp.float32)]
            + [pltpu.SemaphoreType.DMA((PARTS,))] * 8,
            compiler_params=pltpu.CompilerParams(collective_id=0, has_side_effects=True, vmem_limit_bytes=10 * MIB),
        )(code, pair_rows, hidden, h_pair, h_far, h_far_pair, allowed_valid.reshape(1, length), target)
        return probs, logp.reshape(rows_dev)

    row_spec = P(('rep', 'vocab'))
    mat_spec = P(('rep', 'vocab'), None)
    return jax.shard_map(device_step, mesh=mesh, in_specs=(mat_spec, P('vocab', None), P('rep'), P('rep'), row_spec), out_specs=(mat_spec, row_spec), check_vma=False)
```

profile of v0, /device:TPU:0, one launch (start us, length us, event | category | flops | bytes accessed | tf_op | source)
XLA Modules:
  0.0 53.7 jit_solution(1768185017099675489)
XLA Ops:
  0.6 0.0 copy-start
  0.6 0.0 copy-start.1
  0.6 0.0 copy-start.2
  0.7 0.9 %collective-permute-start = (bf16[64,5120]{1,0:T(8,128)(2,1)}, bf16[64,5120]{1,0:T(8,128)(2,1)S(1)}, u32[]{:S(2)}, u32[]{:S(2)}) collective-permute-start(bf16[64,5120]{1,0:T(8,128)(2,1)} %h_own.1), channel_id=1, source_target_pairs={{0,1},{1,0},{2,3},{3,2},{4,5},{5,4},{6,7},{7,6}} | collective-permute-start | bytes 1966088 | tf_op jit(solution)/shard_map/ppermute | solution.py:158
  1.5 2.5 %collective-permute-start.1 = (bf16[64,5120]{1,0:T(8,128)(2,1)}, bf16[64,5120]{1,0:T(8,128)(2,1)S(1)}, u32[]{:S(2)}, u32[]{:S(2)}) collective-permute-start(bf16[64,5120]{1,0:T(8,128)(2,1)} %h_own.1), channel_id=1, source_target_pairs={{0,2},{1,3},{2,0},{3,1},{4,6},{5,7},{6,4},{7,5}} | collective-permute-start | bytes 1966088 | tf_op jit(solution)/shard_map/ppermute | solution.py:157
  4.1 0.7 %add_select_fusion = (s32[2048]{0:T(1024)S(1)}, pred[2048]{0:T(1024)(128)(4,1)S(1)}) fusion(s32[2048]{0:T(1024)} %param.7, s32[]{:T(128)S(6)} %axis_index.12, s32[2048]{0:T(1024)} %param.8), kind=kLoop, calls=%fused_computation | loop fusion | flops 14336 | bytes 26628 | tf_op jit(solution)/shard_map/jit(_where)/select_n | solution.py:164
  4.8 0.7 %and_add_fusion = s32[2048]{0:T(1024)S(1)} fusion(s32[2048]{0:T(1024)} %param.7, pred[2048]{0:T(1024)(128)(4,1)S(1)} %get-tuple-element.22, s32[]{:T(128)S(6)} %axis_index.12), kind=kLoop, calls=%fused_computation.1 | loop fusion | flops 16384 | bytes 18436 | tf_op jit(solution)/shard_map/add | solution.py:163
  5.5 5.0 %sort.14 = (s32[2048]{0:T(1024)S(1)}, s32[2048]{0:T(1024)}) sort(s32[2048]{0:T(1024)S(1)} %and_add_fusion, s32[2048]{0:T(1024)S(1)} %iota.10), dimensions={0}, to_apply=%region_0.1 | sort | flops 22528 | bytes 32768 | tf_op jit(solution)/shard_map/sort | solution.py:163
  10.5 0.0 collective-permute-done.h_pair
  10.5 0.8 %shard_map.68 = bf16[40,2048,2,128]{3,2,1,0:T(2,128)(2,1)S(1)} custom-call(s32[2048]{0:T(1024)S(1)} %get-tuple-element.14.keys, bf16[4096,40,4,2,128]{4,3,2,1,0:T(2,128)(2,1)} %bitcast.4.w), custom_call_target="tpu_custom_call" | custom-call | tf_op jit(solution)/shard_map/pallas_call | solution.py:173
  11.3 8.1 %collective-permute-done.1.h_far = bf16[64,5120]{1,0:T(8,128)(2,1)S(1)} collective-permute-done((bf16[64,5120]{1,0:T(8,128)(2,1)}, bf16[64,5120]{1,0:T(8,128)(2,1)S(1)}, u32[]{:S(2)}, u32[]{:S(2)}) %collective-permute-start.1) | collective-permute-done | bytes 655392 | tf_op jit(solution)/shard_map/ppermute | solution.py:157
  19.4 0.0 collective-permute-start.2
  19.4 2.1 %collective-permute-done.2.h_far_pair = bf16[64,5120]{1,0:T(8,128)(2,1)S(1)} collective-permute-done((bf16[64,5120]{1,0:T(8,128)(2,1)S(1)}, bf16[64,5120]{1,0:T(8,128)(2,1)S(1)}, u32[]{:S(2)}, u32[]{:S(2)}) %collective-permute-start.2) | collective-permute-done | bytes 655392 | tf_op jit(solution)/shard_map/ppermute | solution.py:182
  21.5 0.0 copy-done
  21.5 0.0 copy-done.1
  21.5 0.0 copy-done.2
  21.5 30.8 %shard_map.69 = (f32[64,2048]{1,0:T(8,128)S(1)}, f32[1,64]{1,0:T(1,128)S(1)}) custom-call(s32[1,2048]{1,0:T(1,128)S(1)} %bitcast.12, bf16[40,4096,128]{2,1,0:T(8,128)(2,1)S(1)} %bitcast.10, bf16[64,5120]{1,0:T(8,128)(2,1)S(1)} %copy-done, bf16[64,5120]{1,0:T(8,128)(2,1)S(1)} %collective-permute-done.h_pair, ...), custom_call_target="tpu_custom_call" | custom-call | tf_op jit(solution)/shard_map/pallas_call | solution.py:185
  52.3 0.8 %copy.9 = f32[64,2048]{1,0:T(8,128)} copy(f32[64,2048]{1,0:T(8,128)S(1)} %get-tuple-element.23) | data formatting | bytes 1048576
  53.1 0.5 copy.10
  (1 shorter events, 0.0 us)
Async XLA Ops:
  0.6 20.9 %copy-start = (bf16[64,5120]{1,0:T(8,128)(2,1)S(1)}, bf16[64,5120]{1,0:T(8,128)(2,1)}, u32[]{:S(2)}) copy-start(bf16[64,5120]{1,0:T(8,128)(2,1)} %h_own.1) | copy-start | bytes 1966084
  0.6 20.9 %copy-start.1 = (s32[2048]{0:T(1024)S(1)}, s32[2048]{0:T(1024)}, u32[]{:S(2)}) copy-start(s32[2048]{0:T(1024)} %param.8) | copy-start | bytes 24580
  0.6 20.9 %copy-start.2 = (s32[64]{0:T(128)S(1)}, s32[64]{0:T(128)}, u32[]{:S(2)}) copy-start(s32[64]{0:T(128)} %param.9) | copy-start | bytes 772
  0.7 9.9 %collective-permute-start = (bf16[64,5120]{1,0:T(8,128)(2,1)}, bf16[64,5120]{1,0:T(8,128)(2,1)S(1)}, u32[]{:S(2)}, u32[]{:S(2)}) collective-permute-start(bf16[64,5120]{1,0:T(8,128)(2,1)} %h_own.1), channel_id=1, source_target_pairs={{0,1},{1,0},{2,3},{3,2},{4,5},{5,4},{6,7},{7,6}} | collective-permute-start | bytes 1966088 | tf_op jit(solution)/shard_map/ppermute | solution.py:158
  1.5 17.9 %collective-permute-start.1 = (bf16[64,5120]{1,0:T(8,128)(2,1)}, bf16[64,5120]{1,0:T(8,128)(2,1)S(1)}, u32[]{:S(2)}, u32[]{:S(2)}) collective-permute-start(bf16[64,5120]{1,0:T(8,128)(2,1)} %h_own.1), channel_id=1, source_target_pairs={{0,2},{1,3},{2,0},{3,1},{4,6},{5,7},{6,4},{7,5}} | collective-permute-start | bytes 1966088 | tf_op jit(solution)/shard_map/ppermute | solution.py:157
  19.4 2.1 %collective-permute-start.2 = (bf16[64,5120]{1,0:T(8,128)(2,1)S(1)}, bf16[64,5120]{1,0:T(8,128)(2,1)S(1)}, u32[]{:S(2)}, u32[]{:S(2)}) collective-permute-start(bf16[64,5120]{1,0:T(8,128)(2,1)S(1)} %collective-permute-done.1.h_far), channel_id=1, source_target_pairs={{0,1},{1,0},{2,3},{3,2},{4,5},{5,4},{6,7},{7,6}} | collective-permute-start | bytes 1966088 | tf_op jit(solution)/shard_map/ppermute | solution.py:182
where the time goes:
time: 53.9 us; the launch traced here: 53.7 us
  Pallas kernels  31.6 us (59%)
  waiting for transfers between devices  10.2 us (19%)
  other arithmetic  6.46 us (12%)
  starting transfers between devices  3.4 us (6%)
  local copies, waits for them, and re-layouts  1.32 us (2%)
  between operations  0.68 us (1%)
    pallas_call x1, Pallas kernels, device_step(): pl.pallas_call(score_kernel, out_shape=(pltpu.VMEM((rows_dev, length), jn...  30.8 us
    ppermute x1, waiting for transfers between devices, device_step(): h_far = lax.ppermute(hidden, 'vocab', across)  8.11 us
    sort x1, other arithmetic, device_step(): lax.sort(jnp.where(mine, places, places + length) * vocab_local + lax.bit...  5.04 us
    ppermute x1, starting transfers between devices, device_step(): h_far = lax.ppermute(hidden, 'vocab', across)  2.52 us
    ppermute x1, waiting for transfers between devices, device_step(): h_far_pair = lax.ppermute(h_far, 'vocab', beside)  2.09 us
    unnamed x8, local copies, waits for them, and re-layouts  1.32 us
  transfers between devices with their start and end apart: 3, of which 2 were waited for; matrix products, arithmetic and copies ran while one was open for 12% of the time, Pallas kernels for 1%

commit v1 on v0

--- a/solution.py
+++ b/solution.py
@@ -88,12 +88,14 @@
 
     def part_scores(start):
         at = pl.ds(pl.multiple_of(2 * start, 2 * part), 2 * part)
-        acc = jnp.zeros((2 * part, 2 * LANES), jnp.float32)
-        for k in range(0, ktiles, 2):
-            lhs = jnp.concatenate([rows[k, at], rows[k + 1, at]], axis=1)
-            acc += lax.dot_general(lhs, hidden[:, k * LANES:(k + 2) * LANES], (((1,), (1,)), ((), ())), preferred_element_type=jnp.float32)
-        both[0] = acc[:, :LANES]
-        both[1] = acc[:, LANES:]
+        for t in range(2 * part // 256):
+            at = pl.ds(pl.multiple_of(2 * start + t * 256, 256), 256)
+            acc = jnp.zeros((256, 2 * LANES), jnp.float32)
+            for k in range(0, ktiles, 2):
+                lhs = jnp.concatenate([rows[k, at], rows[k + 1, at]], axis=1)
+                acc += lax.dot_general(lhs, hidden[:, k * LANES:(k + 2) * LANES], (((1,), (1,)), ((), ())), preferred_element_type=jnp.float32)
+            both[0, t * 256:(t + 1) * 256] = acc[:, :LANES]
+            both[1, t * 256:(t + 1) * 256] = acc[:, LANES:]
         kind = jnp.broadcast_to(code[:, pl.ds(pl.multiple_of(start, part), part)], (LANES, part)).T
         picked = []
         for side in range(2):

time: 53.9 us -> 43.2 us (0.80)
  Pallas kernels: 31.6 us -> 20.8 us
    pallas_call x1, Pallas kernels: 30.8 us -> 20 us  [device_step(): pl.pallas_call(score_kernel, out_shape=(pltpu.VMEM((rows_dev, length), jn...]
  transfers between devices with their start and end apart: 3 -> 3, of which waited for: 2 -> 2; matrix products, arithmetic and copies ran while one was open for 12% -> 15% of each run, Pallas kernels for 1% -> 2%
where the time goes in v1:
time: 43.2 us; the launch traced here: 42.9 us
  Pallas kernels  20.8 us (48%)
  waiting for transfers between devices  10.2 us (24%)
  other arithmetic  6.46 us (15%)
  starting transfers between devices  3.4 us (8%)
  local copies, waits for them, and re-layouts  1.32 us (3%)
  between operations  0.68 us (2%)
    pallas_call x1, Pallas kernels, device_step(): pl.pallas_call(score_kernel, out_shape=(pltpu.VMEM((rows_dev, length), jn...  20 us
    ppermute x1, waiting for transfers between devices, device_step(): h_far = lax.ppermute(hidden, 'vocab', across)  8.11 us
    sort x1, other arithmetic, device_step(): lax.sort(jnp.where(mine, places, places + length) * vocab_local + lax.bit...  5.04 us
    ppermute x1, starting transfers between devices, device_step(): h_far = lax.ppermute(hidden, 'vocab', across)  2.52 us
    ppermute x1, waiting for transfers between devices, device_step(): h_far_pair = lax.ppermute(h_far, 'vocab', beside)  2.09 us
    unnamed x8, local copies, waits for them, and re-layouts  1.32 us
    ppermute x1, starting transfers between devices, device_step(): h_pair = lax.ppermute(hidden, 'vocab', beside)  0.88 us
  transfers between devices with their start and end apart: 3, of which 2 were waited for; matrix products, arithmetic and copies ran while one was open for 15% of the time, Pallas kernels for 2%

profile of v1, /device:TPU:0, one launch (start us, length us, event | category | flops | bytes accessed | tf_op | source)
XLA Modules:
  0.0 42.9 jit_solution(13882301272330701966)
XLA Ops:
  0.6 0.0 copy-start
  0.6 0.0 copy-start.1
  0.6 0.0 copy-start.2
  0.7 0.9 %collective-permute-start = (bf16[64,5120]{1,0:T(8,128)(2,1)}, bf16[64,5120]{1,0:T(8,128)(2,1)S(1)}, u32[]{:S(2)}, u32[]{:S(2)}) collective-permute-start(bf16[64,5120]{1,0:T(8,128)(2,1)} %h_own.1), channel_id=1, source_target_pairs={{0,1},{1,0},{2,3},{3,2},{4,5},{5,4},{6,7},{7,6}} | collective-permute-start | bytes 1966088 | tf_op jit(solution)/shard_map/ppermute | solution.py:160
  1.5 2.5 %collective-permute-start.1 = (bf16[64,5120]{1,0:T(8,128)(2,1)}, bf16[64,5120]{1,0:T(8,128)(2,1)S(1)}, u32[]{:S(2)}, u32[]{:S(2)}) collective-permute-start(bf16[64,5120]{1,0:T(8,128)(2,1)} %h_own.1), channel_id=1, source_target_pairs={{0,2},{1,3},{2,0},{3,1},{4,6},{5,7},{6,4},{7,5}} | collective-permute-start | bytes 1966088 | tf_op jit(solution)/shard_map/ppermute | solution.py:159
  4.1 0.7 %add_select_fusion = (s32[2048]{0:T(1024)S(1)}, pred[2048]{0:T(1024)(128)(4,1)S(1)}) fusion(s32[2048]{0:T(1024)} %param.7, s32[]{:T(128)S(6)} %axis_index.12, s32[2048]{0:T(1024)} %param.8), kind=kLoop, calls=%fused_computation | loop fusion | flops 14336 | bytes 26628 | tf_op jit(solution)/shard_map/jit(_where)/select_n | solution.py:166
  4.8 0.7 %and_add_fusion = s32[2048]{0:T(1024)S(1)} fusion(s32[2048]{0:T(1024)} %param.7, pred[2048]{0:T(1024)(128)(4,1)S(1)} %get-tuple-element.22, s32[]{:T(128)S(6)} %axis_index.12), kind=kLoop, calls=%fused_computation.1 | loop fusion | flops 16384 | bytes 18436 | tf_op jit(solution)/shard_map/add | solution.py:165
  5.5 5.0 %sort.14 = (s32[2048]{0:T(1024)S(1)}, s32[2048]{0:T(1024)}) sort(s32[2048]{0:T(1024)S(1)} %and_add_fusion, s32[2048]{0:T(1024)S(1)} %iota.10), dimensions={0}, to_apply=%region_0.1 | sort | flops 22528 | bytes 32768 | tf_op jit(solution)/shard_map/sort | solution.py:165
  10.5 0.0 collective-permute-done.h_pair
  10.5 0.8 %shard_map.68 = bf16[40,2048,2,128]{3,2,1,0:T(2,128)(2,1)S(1)} custom-call(s32[2048]{0:T(1024)S(1)} %get-tuple-element.14.keys, bf16[4096,40,4,2,128]{4,3,2,1,0:T(2,128)(2,1)} %bitcast.4.w), custom_call_target="tpu_custom_call" | custom-call | tf_op jit(solution)/shard_map/pallas_call | solution.py:175
  11.3 8.1 %collective-permute-done.1.h_far = bf16[64,5120]{1,0:T(8,128)(2,1)S(1)} collective-permute-done((bf16[64,5120]{1,0:T(8,128)(2,1)}, bf16[64,5120]{1,0:T(8,128)(2,1)S(1)}, u32[]{:S(2)}, u32[]{:S(2)}) %collective-permute-start.1) | collective-permute-done | bytes 655392 | tf_op jit(solution)/shard_map/ppermute | solution.py:159
  19.4 0.0 collective-permute-start.2
  19.4 2.1 %collective-permute-done.2.h_far_pair = bf16[64,5120]{1,0:T(8,128)(2,1)S(1)} collective-permute-done((bf16[64,5120]{1,0:T(8,128)(2,1)S(1)}, bf16[64,5120]{1,0:T(8,128)(2,1)S(1)}, u32[]{:S(2)}, u32[]{:S(2)}) %collective-permute-start.2) | collective-permute-done | bytes 655392 | tf_op jit(solution)/shard_map/ppermute | solution.py:184
  21.5 0.0 copy-done
  21.5 0.0 copy-done.1
  21.5 0.0 copy-done.2
  21.5 20.0 %shard_map.69 = (f32[64,2048]{1,0:T(8,128)S(1)}, f32[1,64]{1,0:T(1,128)S(1)}) custom-call(s32[1,2048]{1,0:T(1,128)S(1)} %bitcast.12, bf16[40,4096,128]{2,1,0:T(8,128)(2,1)S(1)} %bitcast.10, bf16[64,5120]{1,0:T(8,128)(2,1)S(1)} %copy-done, bf16[64,5120]{1,0:T(8,128)(2,1)S(1)} %collective-permute-done.h_pair, ...), custom_call_target="tpu_custom_call" | custom-call | tf_op jit(solution)/shard_map/pallas_call | solution.py:187
  41.6 0.8 %copy.9 = f32[64,2048]{1,0:T(8,128)} copy(f32[64,2048]{1,0:T(8,128)S(1)} %get-tuple-element.23) | data formatting | bytes 1048576
  42.4 0.5 %copy.10 = f32[64]{0:T(128)} copy(f32[64]{0:T(128)S(1)} %bitcast.14) | data formatting | bytes 512
  (1 shorter events, 0.0 us)
Async XLA Ops:
  0.6 20.9 %copy-start = (bf16[64,5120]{1,0:T(8,128)(2,1)S(1)}, bf16[64,5120]{1,0:T(8,128)(2,1)}, u32[]{:S(2)}) copy-start(bf16[64,5120]{1,0:T(8,128)(2,1)} %h_own.1) | copy-start | bytes 1966084
  0.6 20.9 %copy-start.1 = (s32[2048]{0:T(1024)S(1)}, s32[2048]{0:T(1024)}, u32[]{:S(2)}) copy-start(s32[2048]{0:T(1024)} %param.8) | copy-start | bytes 24580
  0.6 20.9 %copy-start.2 = (s32[64]{0:T(128)S(1)}, s32[64]{0:T(128)}, u32[]{:S(2)}) copy-start(s32[64]{0:T(128)} %param.9) | copy-start | bytes 772
  0.7 9.9 %collective-permute-start = (bf16[64,5120]{1,0:T(8,128)(2,1)}, bf16[64,5120]{1,0:T(8,128)(2,1)S(1)}, u32[]{:S(2)}, u32[]{:S(2)}) collective-permute-start(bf16[64,5120]{1,0:T(8,128)(2,1)} %h_own.1), channel_id=1, source_target_pairs={{0,1},{1,0},{2,3},{3,2},{4,5},{5,4},{6,7},{7,6}} | collective-permute-start | bytes 1966088 | tf_op jit(solution)/shard_map/ppermute | solution.py:160
  1.5 17.9 %collective-permute-start.1 = (bf16[64,5120]{1,0:T(8,128)(2,1)}, bf16[64,5120]{1,0:T(8,128)(2,1)S(1)}, u32[]{:S(2)}, u32[]{:S(2)}) collective-permute-start(bf16[64,5120]{1,0:T(8,128)(2,1)} %h_own.1), channel_id=1, source_target_pairs={{0,2},{1,3},{2,0},{3,1},{4,6},{5,7},{6,4},{7,5}} | collective-permute-start | bytes 1966088 | tf_op jit(solution)/shard_map/ppermute | solution.py:159
  19.4 2.1 %collective-permute-start.2 = (bf16[64,5120]{1,0:T(8,128)(2,1)S(1)}, bf16[64,5120]{1,0:T(8,128)(2,1)S(1)}, u32[]{:S(2)}, u32[]{:S(2)}) collective-permute-start(bf16[64,5120]{1,0:T(8,128)(2,1)S(1)} %collective-permute-done.1.h_far), channel_id=1, source_target_pairs={{0,1},{1,0},{2,3},{3,2},{4,5},{5,4},{6,7},{7,6}} | collective-permute-start | bytes 1966088 | tf_op jit(solution)/shard_map/ppermute | solution.py:184

commit v2 on v0

v2 whole, which is shorter than its diff:
```python
import functools

import jax
import jax.numpy as jnp
from jax import lax
from jax.experimental import pallas as pl
from jax.experimental.pallas import tpu as pltpu
from jax.sharding import PartitionSpec as P

INV_TEMP = 1.25
MESH = pl.DeviceIdType.MESH
LANES = 128
TILE_ROWS = 8
MIB = 1 << 20
ISSUE = 8
PARTS = 8
BLOCK = 256
BAND = 16


def listed(keys, limit):
    length = keys.shape[0]
    low = jnp.int32(0)
    step = length
    while step:
        probe = low + step
        below = keys[jnp.minimum(probe, length) - 1] < limit
        low = jnp.where(below & (probe <= length), probe, low)
        step //= 2
    return low


def gather_kernel(keys, w, pairs, sem, *, row_bits):
    length = keys.shape[0]
    n_groups = lax.div(listed(keys, length << row_bits) + ISSUE - 1, ISSUE)

    def issue(i, carry):
        for u in range(ISSUE):
            key = keys[i * ISSUE + u]
            row = lax.bitwise_and(key, (1 << row_bits) - 1)
            src = w.at[lax.shift_right_logical(row, 3), :, lax.bitwise_and(lax.shift_right_logical(row, 1), 3)]
            spot = lax.bitwise_and(lax.shift_right_logical(key, row_bits), length - 1)
            pltpu.make_async_copy(src, pairs.at[:, spot], sem).start()
        return carry

    lax.fori_loop(0, n_groups, issue, 0)

    def wait(i, carry):
        group = pairs.at[:, pl.ds(0, ISSUE)]
        pltpu.make_async_copy(group, group, sem).wait()
        return carry

    lax.fori_loop(0, n_groups, wait, 0)


def block_dot(rows, at, blocks, first_tile):
    acc = jnp.zeros((BLOCK, sum(block.shape[0] for block in blocks)), jnp.float32)
    for k in range(0, blocks[0].shape[1] // LANES, 2):
        lhs = jnp.concatenate([rows[first_tile + k, at], rows[first_tile + k + 1, at]], axis=1)
        rhs = jnp.concatenate([block[:, k * LANES:(k + 2) * LANES] for block in blocks], axis=0)
        acc += lax.dot_general(lhs, rhs, (((1,), (1,)), ((), ())), preferred_element_type=jnp.float32)
    return acc


def score_kernel(ids, valid, target, rows, h_own, h_pair, h_far, h_far_pair, scores, norm, logp, both,
                 give, got, far_own, far_send, far_recv, g_s, g_r, x_s, x_r, *, row_bits):
    me = lax.axis_index('vocab')
    partner = me + 1 - 2 * lax.rem(me, 2)
    far = me + 2 - 4 * lax.div(me, 2)
    length = valid.shape[1]
    part = length // PARTS
    rows_dev = norm.shape[0]

    barrier = pltpu.get_barrier_semaphore()
    for peer in (partner, far):
        pl.semaphore_signal(barrier, inc=1, device_id={'vocab': peer}, device_id_type=MESH)

    def give_copy(p):
        return pltpu.make_async_remote_copy(src_ref=give.at[p], dst_ref=got.at[p], send_sem=g_s.at[p], recv_sem=g_r.at[p],
                                            device_id={'vocab': partner}, device_id_type=MESH)

    def far_copy(p):
        return pltpu.make_async_remote_copy(src_ref=far_send.at[p], dst_ref=far_recv.at[p], send_sem=x_s.at[p], recv_sem=x_r.at[p],
                                            device_id={'vocab': far}, device_id_type=MESH)

    def compute(p):
        for t in range(2 * part // BLOCK):
            at = pl.ds(pl.multiple_of(p * 2 * part + t * BLOCK, BLOCK), BLOCK)
            here = pl.ds(t * BLOCK, BLOCK)
            acc = block_dot(rows, at, (h_own, h_pair, h_far, h_far_pair), 0)
            both[0, here] = acc[:, :LANES]
            both[1, here] = acc[:, LANES:]
        spots = pl.ds(pl.multiple_of(p * part, part), part)
        ids_part = ids[:, spots]
        kind = jnp.where((lax.shift_right_logical(ids_part, row_bits) == me) & (valid[:, spots] > 0), 1 + lax.bitwise_and(ids_part, 1), 0)
        kind = jnp.broadcast_to(kind, (LANES, part)).T
        flat = []
        for side in range(2):
            even = both[side, pl.ds(0, part, 2), :]
            odd = both[side, pl.ds(1, part, 2), :]
            flat.append(jnp.where(kind == 2, odd, jnp.where(kind == 1, even, 0.0)).T)
        scores[p] = flat[0][:rows_dev]
        far_own[p] = flat[1][:rows_dev]
        give[p, 0] = flat[0][rows_dev:]
        give[p, 1] = flat[1][rows_dev:]

    def merge(p):
        give_copy(p).wait_recv()
        far_send[p] = far_own[p] + got[p, 1]
        far_copy(p).start()
        scores[p] = scores[p] + got[p, 0]

    compute(0)
    pl.semaphore_wait(barrier, 2)
    give_copy(0).start()

    def step(p, carry):
        compute(p)
        give_copy(p).start()
        merge(p - 1)
        return carry

    lax.fori_loop(1, PARTS, step, 0)
    merge(PARTS - 1)
    wanted = jnp.broadcast_to(target[...], (LANES, rows_dev)).T
    wanted = jnp.concatenate([wanted] * (part // LANES), axis=1)
    place = lax.broadcasted_iota(jnp.int32, (rows_dev, part), 1)
    top = jnp.full((rows_dev, part), -jnp.inf, jnp.float32)
    picked = jnp.zeros((rows_dev, part), jnp.float32)
    for p in range(PARTS):
        far_copy(p).wait_recv()
        s = (scores[p] + far_recv[p]) * INV_TEMP
        picked += jnp.where(place + p * part == wanted, s, 0.0)
        s = jnp.where(valid[:, p * part:(p + 1) * part] > 0, s, -jnp.inf)
        scores[p] = s
        top = jnp.maximum(top, s)
    top = jnp.max(top, axis=1, keepdims=True)
    total = jnp.zeros((rows_dev, part), jnp.float32)
    for p in range(PARTS):
        total += jnp.exp(scores[p] - top)
    log_norm = top + jnp.log(jnp.sum(total, axis=1, keepdims=True))
    norm[...] = jnp.broadcast_to(log_norm, (rows_dev, LANES))
    picked = jnp.sum(picked, axis=1, keepdims=True) - log_norm
    logp[...] = jnp.broadcast_to(picked, (rows_dev, LANES)).T[:1, :]
    for p in range(PARTS):
        give_copy(p).wait_send()
        far_copy(p).wait_send()


def finish_kernel(scores, norm, logp, probs_out, logp_out, probs, sem):
    parts, _, part = scores.shape
    bands = probs.shape[0] // BAND
    small = pltpu.make_async_copy(logp, logp_out, sem.at[bands])
    small.start()
    copies = []
    for band in range(bands):
        here = pl.ds(band * BAND, BAND)
        shift = jnp.concatenate([norm[here, :]] * (part // LANES), axis=1)
        for p in range(parts):
            probs[here, p * part:(p + 1) * part] = jnp.exp(scores[p, here] - shift)
        copies.append(pltpu.make_async_copy(probs.at[here], probs_out.at[here], sem.at[band]))
        copies[-1].start()
    for copy in copies:
        copy.wait()
    small.wait()


def solution(mesh):
    shards = mesh.shape['vocab']
    across = [(i, i ^ 2) for i in range(shards)]
    beside = [(i, i ^ 1) for i in range(shards)]

    def device_step(hidden, w_head, allowed_ids, allowed_valid, target_pos):
        rows_dev, depth = hidden.shape
        vocab_local = w_head.shape[0]
        length = allowed_ids.shape[0]
        row_bits = vocab_local.bit_length() - 1
        ktiles = depth // LANES
        h_far = lax.ppermute(hidden, 'vocab', across)
        me = lax.axis_index('vocab')
        mine = (lax.shift_right_logical(allowed_ids, row_bits) == me) & (allowed_valid > 0)
        places = jnp.arange(length, dtype=jnp.int32)
        keys = lax.sort(jnp.where(mine, places, places + length) * vocab_local + lax.bitwise_and(allowed_ids, vocab_local - 1))
        keys, hidden_again = lax.optimization_barrier((keys, hidden))
        h_pair = lax.ppermute(hidden_again, 'vocab', beside)

        w_view = w_head.reshape(vocab_local // TILE_ROWS, TILE_ROWS, ktiles, LANES).transpose(0, 2, 1, 3).reshape(vocab_local // TILE_ROWS, ktiles, TILE_ROWS // 2, 2, LANES)
        any_spec = pl.BlockSpec(memory_space=pl.ANY)
        smem_spec = pl.BlockSpec(memory_space=pltpu.SMEM)
        vmem_spec = pl.BlockSpec(memory_space=pltpu.VMEM)
        pairs = pl.pallas_call(
            functools.partial(gather_kernel, row_bits=row_bits),
            out_shape=pltpu.VMEM((ktiles, length, 2, LANES), jnp.bfloat16),
            in_specs=[smem_spec, any_spec],
            out_specs=vmem_spec,
            scratch_shapes=[pltpu.SemaphoreType.DMA],
            compiler_params=pltpu.CompilerParams(vmem_limit_bytes=2 * MIB),
        )(keys, w_view)
        h_far, pairs = lax.optimization_barrier((h_far, pairs))
        h_far_pair = lax.ppermute(h_far, 'vocab', beside)
        pair_rows = pltpu.with_memory_space_constraint(pairs.reshape(ktiles, 2 * length, LANES), pltpu.VMEM)
        part = length // PARTS
        masked, norm, logp = pl.pallas_call(
            functools.partial(score_kernel, row_bits=row_bits),
            out_shape=(pltpu.VMEM((PARTS, rows_dev, part), jnp.float32), pltpu.VMEM((rows_dev, LANES), jnp.float32), pltpu.VMEM((1, rows_dev), jnp.float32)),
            in_specs=[vmem_spec] * 8,
            out_specs=(vmem_spec,) * 3,
            scratch_shapes=[pltpu.VMEM((2, 2 * part, LANES), jnp.float32)]
            + [pltpu.VMEM((PARTS, 2, rows_dev, part), jnp.float32)] * 2
            + [pltpu.VMEM((PARTS, rows_dev, part), jnp.float32)] * 3
            + [pltpu.SemaphoreType.DMA((PARTS,))] * 4,
            compiler_params=pltpu.CompilerParams(collective_id=0, has_side_effects=True, vmem_limit_bytes=8 * MIB),
        )(allowed_ids.reshape(1, length), allowed_valid.reshape(1, length), target_pos.reshape(1, rows_dev), pair_rows, hidden, h_pair, h_far, h_far_pair)
        masked, norm, logp = (pltpu.with_memory_space_constraint(x, pltpu.VMEM) for x in (masked, norm, logp))
        probs, logp = pl.pallas_call(
            finish_kernel,
            out_shape=(jax.ShapeDtypeStruct((rows_dev, length), jnp.float32), jax.ShapeDtypeStruct((1, rows_dev), jnp.float32)),
            in_specs=[vmem_spec] * 3,
            out_specs=(any_spec, any_spec),
            scratch_shapes=[pltpu.VMEM((rows_dev, length), jnp.float32), pltpu.SemaphoreType.DMA((rows_dev // BAND + 1,))],
        )(masked, norm, logp)
        return probs, logp.reshape(rows_dev)

    row_spec = P(('rep', 'vocab'))
    mat_spec = P(('rep', 'vocab'), None)
    return jax.shard_map(device_step, mesh=mesh, in_specs=(mat_spec, P('vocab', None), P('rep'), P('rep'), row_spec), out_specs=(mat_spec, row_spec), check_vma=False)
```

time: 53.9 us -> 41.8 us (0.78)
  Pallas kernels: 31.6 us -> 21.5 us
  local copies, waits for them, and re-layouts: 1.32 us -> 0.02 us
  other arithmetic: 6.46 us -> 5.76 us
    pallas_call x1 -> x2, Pallas kernels: 30.8 us -> 20.7 us  [the longest x1 19.8 us: device_step(): pl.pallas_call(functools.partial(score_kernel, row_bits=row_bits), out_sh...]
    unnamed x8, local copies, waits for them, and re-layouts: 1.32 us -> 0.02 us
    ppermute x1, starting transfers between devices: 0.88 us -> 0.01 us  [device_step(): h_pair = lax.ppermute(hidden_again, 'vocab', beside)]
    ppermute x1, starting transfers between devices: 2.52 us -> 3.36 us  [device_step(): h_far = lax.ppermute(hidden, 'vocab', across)]
    select_n x1 -> x0, other arithmetic: 0.72 us -> none  [device_step(): jnp.where(mine, 1 + lax.bitwise_and(allowed_ids, 1), 0).reshape(1, length)]
  transfers between devices with their start and end apart: 3 -> 3, of which waited for: 2 -> 2; matrix products, arithmetic and copies ran while one was open for 12% -> 14% of each run, Pallas kernels for 1% -> 2%
where the time goes in v2:
time: 41.8 us; the launch traced here: 41.6 us
  Pallas kernels  21.5 us (51%)
  waiting for transfers between devices  10.3 us (25%)
  other arithmetic  5.76 us (14%)
  starting transfers between devices  3.37 us (8%)
  between operations  0.7 us (2%)
    pallas_call x1, Pallas kernels, device_step(): pl.pallas_call(functools.partial(score_kernel, row_bits=row_bits), out_sh...  19.8 us
    ppermute x1, waiting for transfers between devices, device_step(): h_far = lax.ppermute(hidden, 'vocab', across)  8.18 us
    sort x1, other arithmetic, device_step(): lax.sort(jnp.where(mine, places, places + length) * vocab_local + lax.bit...  5.04 us
    ppermute x1, starting transfers between devices, device_step(): h_far = lax.ppermute(hidden, 'vocab', across)  3.36 us
    ppermute x1, waiting for transfers between devices, device_step(): h_far_pair = lax.ppermute(h_far, 'vocab', beside)  2.09 us
    pallas_call x1, Pallas kernels, device_step(): pl.pallas_call(finish_kernel, out_shape=(jax.ShapeDtypeStruct((rows_dev,...  0.86 us
  transfers between devices with their start and end apart: 3, of which 2 were waited for; matrix products, arithmetic and copies ran while one was open for 14% of the time, Pallas kernels for 2%

profile of v2, /device:TPU:0, one launch (start us, length us, event | category | flops | bytes accessed | tf_op | source)
XLA Modules:
  0.0 41.6 jit_solution(5313934739871911281)
XLA Ops:
  0.6 0.0 copy-start
  0.6 0.0 copy-start.2
  0.7 0.0 copy-start.1
  0.7 0.0 copy-start.3
  0.7 3.4 %collective-permute-start = (bf16[64,5120]{1,0:T(8,128)(2,1)}, bf16[64,5120]{1,0:T(8,128)(2,1)S(1)}, u32[]{:S(2)}, u32[]{:S(2)}) collective-permute-start(bf16[64,5120]{1,0:T(8,128)(2,1)} %h_own.1), channel_id=1, source_target_pairs={{0,2},{1,3},{2,0},{3,1},{4,6},{5,7},{6,4},{7,5}} | collective-permute-start | bytes 1966088 | tf_op jit(solution)/shard_map/ppermute | solution.py:179
  4.0 0.7 %and_add_fusion = s32[2048]{0:T(1024)S(1)} fusion(s32[2048]{0:T(1024)} %param.7, s32[2048]{0:T(1024)} %param.8, s32[]{:T(128)S(6)} %axis_index.12), kind=kLoop, calls=%fused_computation | loop fusion | flops 18432 | bytes 24580 | tf_op jit(solution)/shard_map/add | solution.py:183
  4.8 5.0 %sort.14 = (s32[2048]{0:T(1024)S(1)}, s32[2048]{0:T(1024)}) sort(s32[2048]{0:T(1024)S(1)} %and_add_fusion, s32[2048]{0:T(1024)S(1)} %iota.10), dimensions={0}, to_apply=%region_0.1 | sort | flops 22528 | bytes 32768 | tf_op jit(solution)/shard_map/sort | solution.py:183
  9.8 0.0 collective-permute-start.1
  9.8 0.8 %shard_map.68 = bf16[40,2048,2,128]{3,2,1,0:T(2,128)(2,1)S(1)} custom-call(s32[2048]{0:T(1024)S(1)} %get-tuple-element.14.keys, bf16[4096,40,4,2,128]{4,3,2,1,0:T(2,128)(2,1)} %bitcast.5.w), custom_call_target="tpu_custom_call" | custom-call | tf_op jit(solution)/shard_map/pallas_call | solution.py:191
  10.6 8.2 %collective-permute-done.h_far = bf16[64,5120]{1,0:T(8,128)(2,1)S(1)} collective-permute-done((bf16[64,5120]{1,0:T(8,128)(2,1)}, bf16[64,5120]{1,0:T(8,128)(2,1)S(1)}, u32[]{:S(2)}, u32[]{:S(2)}) %collective-permute-start) | collective-permute-done | bytes 655392 | tf_op jit(solution)/shard_map/ppermute | solution.py:179
  18.8 0.0 collective-permute-start.2
  18.8 0.0 collective-permute-done.1.h_pair
  18.8 2.1 %collective-permute-done.2.h_far_pair = bf16[64,5120]{1,0:T(8,128)(2,1)S(1)} collective-permute-done((bf16[64,5120]{1,0:T(8,128)(2,1)S(1)}, bf16[64,5120]{1,0:T(8,128)(2,1)S(1)}, u32[]{:S(2)}, u32[]{:S(2)}) %collective-permute-start.2) | collective-permute-done | bytes 655392 | tf_op jit(solution)/shard_map/ppermute | solution.py:200
  20.9 0.0 copy-done
  20.9 0.0 copy-done.2
  20.9 0.0 copy-done.1
  20.9 0.0 copy-done.3
  20.9 19.8 %shard_map.69 = (f32[8,64,256]{2,1,0:T(8,128)S(1)}, f32[64,128]{1,0:T(8,128)S(1)}, f32[1,64]{1,0:T(1,128)S(1)}) custom-call(s32[1,2048]{1,0:T(1,128)S(1)} %bitcast.11, s32[1,2048]{1,0:T(1,128)S(1)} %bitcast.12, s32[1,64]{1,0:T(1,128)S(1)} %bitcast.13, bf16[40,4096,128]{2,1,0:T(8,128)(2,1)S(1)} %bitcast.10, bf16[64,5120]{1,0:T(8,128)(2,1)S(1)} %copy-done, ...), custom_call_target="tpu_custom_call" | custom-call | tf_op jit(solution)/shard_map/pallas_call | solution.py:203
  40.7 0.9 %shard_map.70 = (f32[64,2048]{1,0:T(8,128)}, f32[1,64]{1,0:T(1,128)}) custom-call(f32[8,64,256]{2,1,0:T(8,128)S(1)} %get-tuple-element.18.scores, f32[64,128]{1,0:T(8,128)S(1)} %get-tuple-element.19.norm, f32[1,64]{1,0:T(1,128)S(1)} %get-tuple-element.20.logp), custom_call_target="tpu_custom_call" | custom-call | tf_op jit(solution)/shard_map/pallas_call | solution.py:215
  (1 shorter events, 0.0 us)
Async XLA Ops:
  0.6 20.2 %copy-start = (bf16[64,5120]{1,0:T(8,128)(2,1)S(1)}, bf16[64,5120]{1,0:T(8,128)(2,1)}, u32[]{:S(2)}) copy-start(bf16[64,5120]{1,0:T(8,128)(2,1)} %h_own.1) | copy-start | bytes 1966084
  0.6 20.2 %copy-start.2 = (s32[2048]{0:T(1024)S(1)}, s32[2048]{0:T(1024)}, u32[]{:S(2)}) copy-start(s32[2048]{0:T(1024)} %param.8) | copy-start | bytes 24580
  0.7 20.2 %copy-start.1 = (s32[2048]{0:T(1024)S(1)}, s32[2048]{0:T(1024)}, u32[]{:S(2)}) copy-start(s32[2048]{0:T(1024)} %param.7) | copy-start | bytes 24580
  0.7 20.2 %copy-start.3 = (s32[64]{0:T(128)S(1)}, s32[64]{0:T(128)}, u32[]{:S(2)}) copy-start(s32[64]{0:T(128)} %param.9) | copy-start | bytes 772
  0.7 18.1 %collective-permute-start = (bf16[64,5120]{1,0:T(8,128)(2,1)}, bf16[64,5120]{1,0:T(8,128)(2,1)S(1)}, u32[]{:S(2)}, u32[]{:S(2)}) collective-permute-start(bf16[64,5120]{1,0:T(8,128)(2,1)} %h_own.1), channel_id=1, source_target_pairs={{0,2},{1,3},{2,0},{3,1},{4,6},{5,7},{6,4},{7,5}} | collective-permute-start | bytes 1966088 | tf_op jit(solution)/shard_map/ppermute | solution.py:179
  9.8 9.0 %collective-permute-start.1 = (bf16[64,5120]{1,0:T(8,128)(2,1)}, bf16[64,5120]{1,0:T(8,128)(2,1)S(1)}, u32[]{:S(2)}, u32[]{:S(2)}) collective-permute-start(bf16[64,5120]{1,0:T(8,128)(2,1)} %h_own.1), channel_id=1, source_target_pairs={{0,1},{1,0},{2,3},{3,2},{4,5},{5,4},{6,7},{7,6}} | collective-permute-start | bytes 1966088 | tf_op jit(solution)/shard_map/ppermute | solution.py:185
  18.8 2.1 %collective-permute-start.2 = (bf16[64,5120]{1,0:T(8,128)(2,1)S(1)}, bf16[64,5120]{1,0:T(8,128)(2,1)S(1)}, u32[]{:S(2)}, u32[]{:S(2)}) collective-permute-start(bf16[64,5120]{1,0:T(8,128)(2,1)S(1)} %collective-permute-done.h_far), channel_id=1, source_target_pairs={{0,1},{1,0},{2,3},{3,2},{4,5},{5,4},{6,7},{7,6}} | collective-permute-start | bytes 1966088 | tf_op jit(solution)/shard_map/ppermute | solution.py:200
